TPU v7x, 128 devices: a whole 4x4x4 slice. The times are simulated.
128 devices in a mesh: row: 8 (over x, y_hi), col: 16 (over z, y_lo, core).
Axes of the slice: x: 4, y: 4 (y_hi: 2, y_lo: 2; y = y_hi * 2 + y_lo), z: 4, core: 2. Of those that a mesh axis runs over, the one named last changes fastest.
Arguments:
- old_residual: float32 [8192, 16384], P(('row', 'col')), may hold values from -6 to 6
- group_map: int32 [128, 8], replicated, may hold values from 0 to 1023, as said below
- q_factor: float32 [16384, 32], P('col', 'row'), may hold values from -0.046875 to 0.046875
Outputs:
- relaid: float32 [8192, 16384], P('row', 'col')
- projection: float32 [32, 8192], P(None, ('row', 'col'))
- row_norms: float32 [8192], P(('row', 'col'))
Inputs may be any that keep to these rules, and one draw needn't show every extreme that they name: `group_map`: all entries together are each group id 0 to 1023 once; row d (old device d) holds exactly one id of each range k * 128 to (k + 1) * 128 - 1, in any slot order.
All inputs are finite; a program needn't handle non-finite values.
Results may differ from a plain program's by a relative error of at most 0.00007.
Values sent between devices are 32-bit elements; how exact they have to be, the bound alone decides.
A program may use at most 64 MiB of HBM per device.

v0:
```python
import jax
import jax.numpy as jnp
from jax import lax
from jax.sharding import PartitionSpec as P

epsilon = 1e-06


def sent_to_all(shard, axis):
    count = lax.axis_size(axis)
    return lax.all_to_all(
        jnp.broadcast_to(shard[None], (count, *shard.shape)), axis, 0, 0, tiled=True
    )


def laid_out(tiles, dim):
    tiles = jnp.moveaxis(tiles, 0, dim)
    shape = tiles.shape
    return tiles.reshape(*shape[:dim], shape[dim] * shape[dim + 1], *shape[dim + 2 :])


def gathered_copies(shard, axis, dim):
    tiles = sent_to_all(shard, axis)
    return laid_out(tiles, dim)


def cut_along(shard, dim, count):
    before, after = (shard.shape[:dim], shard.shape[dim + 1 :])
    return jnp.moveaxis(shard.reshape(*before, count, -1, *after), dim, 0)


def sum_at_owner(shard, axis, dim):
    count = lax.axis_size(axis)
    tiles = lax.all_to_all(cut_along(shard, dim, count), axis, 0, 0, tiled=True)
    return jnp.sum(tiles, axis=0)


def on_device(old_residual, group_map, q_factor):
    row_count = lax.axis_size("row")
    column_count = lax.axis_size("col")
    devices_all = row_count * column_count
    my_row = lax.axis_index("row")
    my_column = lax.axis_index("col")
    position = my_row * column_count + my_column
    group_rows = old_residual.shape[0] // row_count
    full_width = old_residual.shape[1]
    block_width = full_width // column_count
    own_ids = lax.dynamic_index_in_dim(group_map, position, 0, keepdims=False)
    sending = jnp.argsort(own_ids)
    stored = jnp.take(old_residual.reshape(row_count, group_rows, full_width), sending, axis=0)
    pieces = stored.reshape(row_count, group_rows, column_count, block_width).transpose(0, 2, 1, 3)
    flat_pieces = pieces.reshape(devices_all, group_rows, block_width)
    received = lax.all_to_all(flat_pieces, ("row", "col"), split_axis=0, concat_axis=0, tiled=True)
    sorted_map = jnp.sort(group_map, axis=1)
    arriving_ids = lax.dynamic_index_in_dim(sorted_map, my_row, 1, keepdims=False)
    placement = jnp.argsort(arriving_ids)
    arranged = jnp.take(received, placement, axis=0)
    relaid_block = arranged.reshape(devices_all * group_rows, block_width)
    factor_full = gathered_copies(q_factor, "row", 1)
    projected_share = sum_at_owner(
        jnp.dot(
            relaid_block,
            factor_full,
            precision=lax.Precision.HIGHEST,
            preferred_element_type=jnp.float32,
        ),
        "col",
        0,
    )
    squares = jnp.sum(relaid_block * relaid_block, axis=1)
    square_total = sum_at_owner(squares, "col", 0)
    row_norms = jnp.sqrt(square_total / full_width + epsilon)
    return (relaid_block, projected_share.T, row_norms)


def solution(mesh):
    placed = (P(("row", "col"), None), P(), P("col", "row"))
    return jax.shard_map(
        on_device,
        mesh=mesh,
        in_specs=placed,
        out_specs=(P("row", "col"), P(None, ("row", "col")), P(("row", "col"))),
        check_vma=False,
    )
```

profile of v0, /device:TPU:1, one launch (start us, length us, event | category | flops | bytes accessed | tf_op | source)
XLA Modules:
  0.0 125.2 jit_solution(10341393157861966837)
XLA Ops:
  0.6 1.4 %broadcast_in_dim.59 = f32[8,1024,4]{1,2,0:T(4,128)} broadcast(f32[1024,4]{0,1:T(4,128)} %param.5), dimensions={1,2} | broadcast | bytes 147456 | tf_op jit(solution)/shard_map/broadcast_in_dim | solution.py:12
  2.0 7.5 %all-to-all-start.1 = ((f32[8,1024,4]{1,2,0:T(4,128)}), f32[8,1024,4]{1,2,0:T(4,128)S(1)}, u32[]{:S(2)}, u32[]{:S(2)}) async-start(f32[8,1024,4]{1,2,0:T(4,128)} %broadcast_in_dim.59), calls=%async_computation.1 | async-start | bytes 262144 | tf_op jit(solution)/shard_map/all_to_all | solution.py:11
  9.5 0.9 dynamic-slice_reduce_fusion
  10.3 1.0 sort.51
  11.3 5.0 %gather_fusion = f32[8,8,16384]{2,1,0:T(8,128)} fusion(f32[8,8,16384]{2,1,0:T(8,128)} %bitcast.26, s32[1024]{0:T(1024)S(1)} %pad_clamp_fusion.1), kind=kCustom, calls=%fused_computation | custom fusion | bytes 8388640 | tf_op jit(solution)/shard_map/jit(_take)/gather | solution.py:50
  16.4 5.1 %broadcast_select_fusion.1 = f32[8,8,16,1024]{3,1,2,0:T(8,128)} fusion(f32[8,8,16,1024]{3,1,2,0:T(8,128)} %bitcast.25, pred[8]{0:T(512)(128)(4,1)S(1)} %compare_and_fusion), kind=kLoop, calls=%fused_computation.5 | loop fusion | flops 1048576 | bytes 8388616 | tf_op jit(solution)/shard_map/jit(_take)/select_n | solution.py:50
  21.5 0.0 all-to-all-done.1
  21.5 11.7 %all-to-all-start = ((f32[128,8,1024]{2,1,0:T(8,128)}), f32[128,8,1024]{2,1,0:T(8,128)}, u32[]{:S(2)}, u32[]{:S(2)}) async-start(f32[128,8,1024]{2,1,0:T(8,128)} %bitcast.23), calls=%async_computation | async-start | bytes 8388608 | tf_op jit(solution)/shard_map/all_to_all | solution.py:53
  33.2 0.0 copy-done.1
  33.2 0.7 sort.49
  33.8 2.5 %sort.50 = (s32[128]{0:T(128)}, s32[128]{0:T(128)S(1)}) sort(s32[128]{0:T(128)S(1)} %dynamic-slice_bitcast_fusion, s32[128]{0:T(128)S(1)} %iota.12), dimensions={0}, to_apply=%region_1.2 | sort | flops 896 | bytes 2048 | tf_op jit(solution)/shard_map/jit(argsort)/sort | solution.py:56
  36.4 0.1 broadcast_in_dim.54
  36.5 0.1 broadcast_in_dim.46
  36.6 0.1 broadcast_in_dim.47
  36.7 0.1 broadcast_bitcast_fusion
  36.8 49.1 %all-to-all-done = f32[128,8,1024]{2,1,0:T(8,128)} async-done(((f32[128,8,1024]{2,1,0:T(8,128)}), f32[128,8,1024]{2,1,0:T(8,128)}, u32[]{:S(2)}, u32[]{:S(2)}) %all-to-all-start) | async-done | bytes 4194336 | tf_op jit(solution)/shard_map/all_to_all | solution.py:53
  85.9 5.0 %gather_fusion.1 = f32[128,8,1024]{2,1,0:T(8,128)} fusion(f32[128,8,1024]{2,1,0:T(8,128)} %all-to-all-done, s32[1024]{0:T(1024)S(1)} %pad_clamp_fusion), kind=kCustom, calls=%fused_computation.1 | custom fusion | bytes 8389120 | tf_op jit(solution)/shard_map/jit(_take)/gather | solution.py:57
  90.9 4.7 %bitcast_select_fusion = f32[1024,1024]{1,0:T(8,128)} fusion(f32[128,8,1024]{2,1,0:T(8,128)} %gather_fusion.1, pred[1024]{0:T(1024)(128)(4,1)S(1)} %broadcast_in_dim.47), kind=kLoop, calls=%fused_computation.2 | loop fusion | flops 1048576 | bytes 8389632 | tf_op jit(solution)/shard_map/jit(_take)/select_n | solution.py:57
  95.6 0.0 copy-done
  95.6 2.4 %multiply_reduce_fusion = (f32[128,8]{1,0:T(8,128)S(1)}, f32[128,8,1024]{2,1,0:T(8,128)}) fusion(f32[128,8,1024]{2,1,0:T(8,128)S(1)} %copy-done, pred[128]{0:T(512)(128)(4,1)S(1)} %compare_and_fusion.1, pred[128,8]{1,0:T(8,128)(4,1)S(1)} %broadcast_bitcast_fusion), kind=kLoop, calls=%fused_computation.3 | loop fusion | flops 4193280 | bytes 8393856 | tf_op jit(solution)/shard_map/reduce_sum | solution.py:70
  98.1 0.7 all_to_all.18
  98.7 4.2 %all-to-all-start.3 = ((f32[16,1,64]{2,1,0:T(1,128)}), f32[16,1,64]{2,1,0:T(1,128)S(1)}, u32[]{:S(2)}, u32[]{:S(2)}) async-start(f32[16,1,64]{2,1,0:T(1,128)} %bitcast.10), calls=%async_computation.3 | async-start | bytes 16384 | tf_op jit(solution)/shard_map/all_to_all | solution.py:34
  102.9 7.4 %convolution_bitcast_fusion = f32[16,32,64]{2,1,0:T(8,128)S(1)} fusion(f32[16,64,1024]{2,1,0:T(8,128)} %bitcast.24, f32[1024,32,1]{0,1,2:T(8,128)S(1)} %reshape.103), kind=kOutput, calls=%fused_computation.16 | convolution fusion | flops 402653184 | bytes 4456448 | tf_op jit(solution)/shard_map/dot_general | solution.py:61
  110.3 0.8 reshape.106
  111.1 0.0 all-to-all-done.3
  111.1 5.8 %all-to-all-start.2 = ((f32[16,1,2048]{2,1,0:T(1,128)}), f32[16,1,2048]{2,1,0:T(1,128)S(1)}, u32[]{:S(2)}, u32[]{:S(2)}) async-start(f32[16,1,2048]{2,1,0:T(1,128)} %reshape.106), calls=%async_computation.2 | async-start | bytes 262144 | tf_op jit(solution)/shard_map/all_to_all | solution.py:34
  117.0 0.5 add_sqrt_fusion
  117.5 5.6 %all-to-all-done.2 = f32[16,1,2048]{2,1,0:T(1,128)S(1)} async-done(((f32[16,1,2048]{2,1,0:T(1,128)}), f32[16,1,2048]{2,1,0:T(1,128)S(1)}, u32[]{:S(2)}, u32[]{:S(2)}) %all-to-all-start.2) | async-done | bytes 131104 | tf_op jit(solution)/shard_map/all_to_all | solution.py:34
  123.0 0.5 broadcast.61
  123.5 0.9 reduce.4
  124.5 0.1 reshape.107
  124.6 0.6 bitcast_reduce_fusion
  (14 shorter events, 0.1 us)
Async XLA Ops:
  2.0 19.5 %all-to-all-start.1 = ((f32[8,1024,4]{1,2,0:T(4,128)}), f32[8,1024,4]{1,2,0:T(4,128)S(1)}, u32[]{:S(2)}, u32[]{:S(2)}) async-start(f32[8,1024,4]{1,2,0:T(4,128)} %broadcast_in_dim.59), calls=%async_computation.1 | async-start | bytes 262144 | tf_op jit(solution)/shard_map/all_to_all | solution.py:11
  21.5 11.7 %copy-start.1 = (s32[128,8]{0,1:T(8,128)S(1)}, s32[128,8]{0,1:T(8,128)}, u32[]{:S(2)}) copy-start(s32[128,8]{0,1:T(8,128)} %param.4) | copy-start | bytes 12292
  21.5 64.5 %all-to-all-start = ((f32[128,8,1024]{2,1,0:T(8,128)}), f32[128,8,1024]{2,1,0:T(8,128)}, u32[]{:S(2)}, u32[]{:S(2)}) async-start(f32[128,8,1024]{2,1,0:T(8,128)} %bitcast.23), calls=%async_computation | async-start | bytes 8388608 | tf_op jit(solution)/shard_map/all_to_all | solution.py:53
  90.9 4.7 %copy-start = (f32[128,8,1024]{2,1,0:T(8,128)S(1)}, f32[128,8,1024]{2,1,0:T(8,128)}, u32[]{:S(2)}) copy-start(f32[128,8,1024]{2,1,0:T(8,128)} %gather_fusion.1) | copy-start | bytes 12582916
  98.7 12.4 %all-to-all-start.3 = ((f32[16,1,64]{2,1,0:T(1,128)}), f32[16,1,64]{2,1,0:T(1,128)S(1)}, u32[]{:S(2)}, u32[]{:S(2)}) async-start(f32[16,1,64]{2,1,0:T(1,128)} %bitcast.10), calls=%async_computation.3 | async-start | bytes 16384 | tf_op jit(solution)/shard_map/all_to_all | solution.py:34
  111.1 11.9 %all-to-all-start.2 = ((f32[16,1,2048]{2,1,0:T(1,128)}), f32[16,1,2048]{2,1,0:T(1,128)S(1)}, u32[]{:S(2)}, u32[]{:S(2)}) async-start(f32[16,1,2048]{2,1,0:T(1,128)} %reshape.106), calls=%async_computation.2 | async-start | bytes 262144 | tf_op jit(solution)/shard_map/all_to_all | solution.py:34
where the time goes:
time: 126 us; the launch traced here: 125 us
  waiting for transfers between devices  54.6 us (43%)
  starting transfers between devices  29.1 us (23%)
  other arithmetic  18.6 us (15%)
  local copies, waits for them, and re-layouts  14.8 us (12%)
  matrix products  7.39 us (6%)
    all_to_all x1, waiting for transfers between devices, on_device(): lax.all_to_all(flat_pieces, ('row', 'col'), split_axis=0, concat_axis=0,...  49.1 us
    all_to_all x1, starting transfers between devices, on_device(): lax.all_to_all(flat_pieces, ('row', 'col'), split_axis=0, concat_axis=0,...  11.7 us
    all_to_all x2, starting transfers between devices, sum_at_owner(): tiles = lax.all_to_all(cut_along(shard, dim, count), axis, 0, 0, tiled=True)  9.96 us
    all_to_all x1, starting transfers between devices, sent_to_all(): lax.all_to_all(jnp.broadcast_to(shard[None], (count, *shard.shape)), axis...  7.47 us
    dot_general x1, matrix products, on_device(): jnp.dot(relaid_block, factor_full, precision=lax.Precision.HIGHEST, prefe...  7.39 us
    all_to_all x2, waiting for transfers between devices, sum_at_owner(): tiles = lax.all_to_all(cut_along(shard, dim, count), axis, 0, 0, tiled=True)  5.55 us
    select_n x2, other arithmetic, on_device(): jnp.take(old_residual.reshape(row_count, group_rows, full_width), sending...  5.11 us
    gather x1, local copies, waits for them, and re-layouts, on_device(): jnp.take(old_residual.reshape(row_count, group_rows, full_width), sending...  5.02 us
  transfers between devices with their start and end apart: 4, of which 2 were waited for; matrix products, arithmetic and copies ran while one was open for 19% of the time, Pallas kernels for 0%

commit v1 on v0

v1 whole, which is shorter than its diff:
```python
import functools

import jax
import jax.numpy as jnp
from jax import lax
from jax.experimental import pallas as pl
from jax.experimental.pallas import tpu as pltpu
from jax.sharding import PartitionSpec as P

epsilon = 1e-06
MESH = pl.DeviceIdType.MESH
ROWS, COLS = 8, 16
DEVS = ROWS * COLS
CHUNK = 8
CHUNKS = DEVS // CHUNK
STEP = 51


def place():
    row, col = lax.axis_index("row"), lax.axis_index("col")
    return row, col


def shifted(row, col, n, sign):
    o = lax.rem(STEP * (n + 1), DEVS)
    bit = lambda i: lax.rem(lax.div(o, 2**i), 2)
    dx = bit(0) + 2 * bit(3)
    dy = bit(1) + 2 * bit(4)
    dz = bit(2) + 2 * bit(5)
    dk = bit(6)
    x = lax.div(row, 2)
    y = lax.rem(row, 2) * 2 + lax.rem(lax.div(col, 2), 2)
    z = lax.div(col, 4)
    k = lax.rem(col, 2)
    x = lax.rem(x + 4 + sign * dx, 4)
    y = lax.rem(y + 4 + sign * dy, 4)
    z = lax.rem(z + 4 + sign * dz, 4)
    k = lax.rem(k + dk, 2)
    return x * 2 + lax.div(y, 2), z * 4 + lax.rem(y, 2) * 2 + k


def kernel(
    old, gmap_s, gmap_v, q_own, relaid, p_out, norm_out,
    stage, send, recv, q_all, w_rows, w, p_part, s_part, p_send, p_recv, inv_v, inv_s,
    in_sem, inv_sem, q_ssem, q_rsem, ssem, rsem, p_ssem, p_rsem,
):
    row, col = place()
    me = row * COLS + col
    for j in range(ROWS):
        pltpu.make_async_copy(old.at[j], stage.at[j], in_sem.at[j]).start()

    barrier = pltpu.get_barrier_semaphore()

    @pl.loop(1, DEVS)
    def _(i):
        peer = lax.rem(me + i, DEVS)
        pl.semaphore_signal(
            barrier, inc=1, device_id=(lax.div(peer, COLS), lax.rem(peer, COLS)), device_id_type=MESH
        )

    slots = []
    for k in range(ROWS):
        slot = jnp.int32(0)
        for j in range(ROWS):
            slot += jnp.where(lax.shift_right_arithmetic(gmap_s[j, me], 7) == k, j, 0)
        slots.append(lax.bitwise_and(slot, 7))
    for j in range(ROWS):
        pltpu.make_async_copy(old.at[j], stage.at[j], in_sem.at[j]).wait()
    for k in range(ROWS):
        for c in range(COLS):
            send[k * COLS + c] = stage[slots[k], :, c * 1024 : (c + 1) * 1024]
    pl.semaphore_wait(barrier, DEVS - 1)

    @pl.loop(1, ROWS)
    def _(r):
        pltpu.make_async_remote_copy(
            src_ref=q_own, dst_ref=q_all.at[row], send_sem=q_ssem, recv_sem=q_rsem,
            device_id=(lax.rem(row + r, ROWS), col), device_id_type=MESH,
        ).start()

    @pl.loop(0, DEVS - 1)
    def _(n):
        r, c = shifted(row, col, n, 1)
        pltpu.make_async_remote_copy(
            src_ref=send.at[r * COLS + c], dst_ref=recv.at[me], send_sem=ssem,
            recv_sem=rsem.at[lax.div(n, CHUNK)], device_id=(r, c), device_id_type=MESH,
        ).start()

    recv[me] = send[me]
    q_all[row] = q_own[...]

    ids = gmap_v[...]
    mine = lax.shift_right_arithmetic(ids, 7) == row
    where_to = jnp.sum(jnp.where(mine, lax.bitwise_and(ids, 127), 0), axis=0, keepdims=True)
    spread = jnp.transpose(jnp.broadcast_to(where_to, (DEVS, DEVS)))
    lanes = lax.broadcasted_iota(jnp.int32, (DEVS, DEVS), 1)
    sources = lax.broadcasted_iota(jnp.int32, (DEVS, DEVS), 0)
    inverse = jnp.sum(jnp.where(spread == lanes, sources, 0), axis=0, keepdims=True)
    inv_v[...] = jnp.broadcast_to(lax.bitwise_and(inverse, 127), (8, DEVS))
    pltpu.make_async_copy(inv_v, inv_s, inv_sem).start()

    q7 = q_all.at[pl.ds(0, ROWS - 1)]
    pltpu.make_async_remote_copy(
        src_ref=q7, dst_ref=q7, send_sem=q_ssem, recv_sem=q_rsem, device_id=(row, col), device_id_type=MESH
    ).wait()
    for r in range(ROWS):
        for i in range(4):
            w_rows[32 * i + 4 * r : 32 * i + 4 * r + 4, :] = q_all[r]
    w[...] = jnp.transpose(w_rows[...])

    def multiply(i):
        blocks, at = [], []
        for j in range(CHUNK):
            r, c = shifted(row, col, i * CHUNK + j, -1)
            at.append(r * COLS + c)
            blocks.append(recv[at[-1]])
        rows = jnp.concatenate(blocks, axis=0)
        part = jnp.dot(rows, w[...], precision=lax.Precision.HIGHEST, preferred_element_type=jnp.float32)
        squares = jnp.sum(rows * rows, axis=1, keepdims=True)
        for j in range(CHUNK):
            p_part[at[j]] = part[8 * j : 8 * j + 8]
            s_part[at[j]] = jnp.broadcast_to(squares[8 * j : 8 * j + 8], (8, 128))

    def arrived(i, count):
        v = recv.at[pl.ds(0, count)]
        pltpu.make_async_remote_copy(
            src_ref=v, dst_ref=v, send_sem=ssem, recv_sem=rsem.at[i], device_id=(row, col), device_id_type=MESH
        ).wait_recv()

    @pl.loop(0, CHUNKS - 1)
    def _(i):
        arrived(i, CHUNK)
        multiply(i)

    arrived(CHUNKS - 1, CHUNK - 1)
    multiply(CHUNKS - 1)

    pltpu.make_async_copy(inv_v, inv_s, inv_sem).wait()
    lane = lax.broadcasted_iota(jnp.int32, (8, 128), 1)

    @pl.loop(0, COLS)
    def _(c):
        for t in range(2):
            tile = p_part[inv_s[0, c * 8 + t * 4]]
            for i in range(1, 4):
                tile = jnp.where(lane < 32 * i, tile, p_part[inv_s[0, c * 8 + t * 4 + i]])
            p_send[c, t] = tile
        tile = s_part[inv_s[0, c * 8]]
        for i in range(1, 8):
            tile = jnp.where(lane < 16 * i, tile, s_part[inv_s[0, c * 8 + i]])
        p_send[c, 2] = tile

    @pl.loop(1, COLS)
    def _(i):
        c = lax.rem(col + i, COLS)
        pltpu.make_async_remote_copy(
            src_ref=p_send.at[c], dst_ref=p_recv.at[col], send_sem=p_ssem, recv_sem=p_rsem,
            device_id=(row, c), device_id_type=MESH,
        ).start()

    p_recv[col] = p_send[col]

    @pl.loop(0, DEVS, unroll=8)
    def _(p):
        relaid[p] = recv[inv_s[0, p]]

    p15 = p_recv.at[pl.ds(0, COLS - 1)]
    pltpu.make_async_remote_copy(
        src_ref=p15, dst_ref=p15, send_sem=p_ssem, recv_sem=p_rsem, device_id=(row, col), device_id_type=MESH
    ).wait()
    total = p_recv[0]
    for c in range(1, COLS):
        total = total + p_recv[c]
    rows = []
    for g in range(8):
        t, i = divmod(g, 4)
        values = total[t] if i == 0 else pltpu.roll(total[t], 128 - 32 * i, axis=1)
        norms = pltpu.roll(total[2], (128 + 32 - 16 * g) % 128, axis=1) if g != 2 else total[2]
        rows.append(jnp.where(lane < 32, values, norms))
    flat = jnp.concatenate(rows + rows, axis=0)
    turned = jnp.transpose(flat)
    p_out[...] = turned[0:32, 0:64]
    norm_out[...] = jnp.sqrt(turned[32:33, 0:64] / 16384.0 + epsilon)

    v = recv.at[pl.ds(0, DEVS - 1)]
    pltpu.make_async_remote_copy(
        src_ref=v, dst_ref=v, send_sem=ssem, recv_sem=rsem.at[0], device_id=(row, col), device_id_type=MESH
    ).wait_send()


def on_device(old_residual, group_map, q_factor):
    f32 = jnp.float32
    ids = group_map.T
    vmem = pl.BlockSpec(memory_space=pltpu.VMEM)
    dma = pltpu.SemaphoreType.DMA
    relaid, projection, norms = pl.pallas_call(
        kernel,
        out_shape=(
            jax.ShapeDtypeStruct((DEVS, 8, 1024), f32),
            jax.ShapeDtypeStruct((32, 64), f32),
            jax.ShapeDtypeStruct((1, 64), f32),
        ),
        in_specs=[
            pl.BlockSpec(memory_space=pl.ANY),
            pl.BlockSpec(memory_space=pltpu.SMEM),
            vmem,
            vmem,
        ],
        out_specs=(vmem, vmem, vmem),
        scratch_shapes=[
            pltpu.VMEM((ROWS, 8, 16384), f32),
            pltpu.VMEM((DEVS, 8, 1024), f32),
            pltpu.VMEM((DEVS, 8, 1024), f32),
            pltpu.VMEM((ROWS, 4, 1024), f32),
            pltpu.VMEM((128, 1024), f32),
            pltpu.VMEM((1024, 128), f32),
            pltpu.VMEM((DEVS, 8, 128), f32),
            pltpu.VMEM((DEVS, 8, 128), f32),
            pltpu.VMEM((COLS, 3, 8, 128), f32),
            pltpu.VMEM((COLS, 3, 8, 128), f32),
            pltpu.VMEM((8, 128), jnp.int32),
            pltpu.SMEM((8, 128), jnp.int32),
            dma((ROWS,)),
            dma,
            dma,
            dma,
            dma,
            dma((CHUNKS,)),
            dma,
            dma,
        ],
        compiler_params=pltpu.CompilerParams(
            collective_id=0, has_side_effects=True, vmem_limit_bytes=48 << 20
        ),
    )(old_residual.reshape(ROWS, 8, 16384), ids, ids, q_factor.T)
    return relaid.reshape(1024, 1024), projection, norms.reshape(64)


def solution(mesh):
    return jax.shard_map(
        on_device,
        mesh=mesh,
        in_specs=(P(("row", "col"), None), P(), P("col", "row")),
        out_specs=(P("row", "col"), P(None, ("row", "col")), P(("row", "col"))),
        check_vma=False,
    )
```

time: 126 us -> 72.1 us (0.57)
  Pallas kernels: 0 us -> 66.7 us
  waiting for transfers between devices: 54.6 us -> 0 us
  starting transfers between devices: 29.1 us -> 0 us
  other arithmetic: 18.6 us -> 0 us
  local copies, waits for them, and re-layouts: 14.8 us -> 4.53 us
  matrix products: 7.39 us -> 0 us
    pallas_call x0 -> x1, Pallas kernels: none -> 66.7 us  [on_device(): pl.pallas_call(kernel, out_shape=(jax.ShapeDtypeStruct((DEVS, 8, 1024), f...]
    all_to_all x4 -> x0, waiting for transfers between devices: 54.6 us -> none  [the longest x1 49.1 us: on_device(): lax.all_to_all(flat_pieces, ('row', 'col'), split_axis=0, concat_axis=0,...]
    all_to_all x4 -> x0, starting transfers between devices: 29.1 us -> none  [the longest x1 11.7 us: on_device(): lax.all_to_all(flat_pieces, ('row', 'col'), split_axis=0, concat_axis=0,...]
    gather x2 -> x0, local copies, waits for them, and re-layouts: 9.99 us -> none  [the longest x1 5.02 us: on_device(): jnp.take(old_residual.reshape(row_count, group_rows, full_width), sending...]
    select_n x4 -> x0, other arithmetic: 9.82 us -> none  [the longest x2 5.11 us: on_device(): jnp.take(old_residual.reshape(row_count, group_rows, full_width), sending...]
    dot_general x1 -> x0, matrix products: 7.39 us -> none  [on_device(): jnp.dot(relaid_block, factor_full, precision=lax.Precision.HIGHEST, prefe...]
    sort x3 -> x0, other arithmetic: 4.15 us -> none  [the longest x1 2.54 us: on_device(): placement = jnp.argsort(arriving_ids)]
    unnamed x6 -> x7, local copies, waits for them, and re-layouts: 0.93 us -> 4.53 us
  transfers between devices with their start and end apart: 4 -> 0, of which waited for: 2 -> 0; matrix products, arithmetic and copies ran while one was open for 19% -> 0% of each run, Pallas kernels for 0% -> 0%
where the time goes in v1:
time: 72.1 us; the launch traced here: 71.9 us
  Pallas kernels  66.7 us (93%)
  local copies, waits for them, and re-layouts  4.53 us (6%)
    pallas_call x1, Pallas kernels, on_device(): pl.pallas_call(kernel, out_shape=(jax.ShapeDtypeStruct((DEVS, 8, 1024), f...  66.7 us
    unnamed x7, local copies, waits for them, and re-layouts  4.53 us

profile of v1, /device:TPU:1, one launch (start us, length us, event | category | flops | bytes accessed | tf_op | source)
XLA Modules:
  0.0 71.9 jit_solution(6340151315807880762)
XLA Ops:
  0.6 0.0 copy-start
  0.6 0.7 copy-done
  1.3 0.0 copy-start.1
  1.4 0.7 copy-done.1
  2.0 66.7 %shard_map.58 = (f32[128,8,1024]{2,1,0:T(8,128)S(1)}, f32[32,64]{1,0:T(8,128)S(1)}, f32[1,64]{1,0:T(1,128)S(1)}) custom-call(f32[8,8,16384]{2,1,0:T(8,128)} %bitcast.10, s32[8,128]{1,0:T(8,128)S(1)} %bitcast.7, s32[8,128]{1,0:T(8,128)S(1)} %bitcast.8, f32[4,1024]{1,0:T(4,128)S(1)} %bitcast.6), custom_call_target="tpu_custom_call" | custom-call | tf_op jit(solution)/shard_map/pallas_call | solution.py:196
  68.7 2.0 %copy.9 = f32[1024,1024]{1,0:T(8,128)} copy(f32[1024,1024]{1,0:T(8,128)S(1)} %bitcast.5) | data formatting | bytes 8388608
  70.8 0.6 copy.10
  71.4 0.5 copy.11
Async XLA Ops:
  0.6 0.7 copy-start
  1.3 0.7 copy-start.1

commit v2 on v0

v2 whole, which is shorter than its diff:
```python
import jax
import jax.numpy as jnp
from jax import lax
from jax.experimental import pallas as pl
from jax.experimental.pallas import tpu as pltpu
from jax.sharding import PartitionSpec as P

epsilon = 1e-06
MESH = pl.DeviceIdType.MESH
ROWS, COLS = 8, 16
DEVS = ROWS * COLS
CHUNK = 8
CHUNKS = DEVS // CHUNK


def order():
    offsets = []
    for n in range(DEVS):
        c = 1 + MULT_C * n % 15 if n < DEVS - ROWS else 0
        s = MULT_S * (n + 1) % ROWS
        v = {name: c >> i & 1 for i, name in enumerate(BITS_C)} | {name: s >> i & 1 for i, name in enumerate(BITS_S)}
        offsets.append((v["x0"] + 2 * v["x1"], v["y0"] + 2 * v["y1"], v["z0"] + 2 * v["z1"], v["k"]))
    return offsets


MULT_C, MULT_S = 7, 3
BITS_C, BITS_S = ("z0", "z1", "y0", "k"), ("x0", "x1", "y1")
EARLY = 96
ORDER = order()
HOPS = (0, 1, 2, 1)


class Place:
    def __init__(self):
        row, col = lax.axis_index("row"), lax.axis_index("col")
        x, z, core = lax.div(row, 2), lax.div(col, 4), lax.rem(col, 2)
        y = lax.rem(row, 2) * 2 + lax.rem(lax.div(col, 2), 2)
        ys = [lax.rem(y + d, 4) for d in range(4)]
        self.row, self.col, self.me = row, col, row * COLS + col
        self.x_row = [2 * lax.rem(x + d, 4) for d in range(4)]
        self.y_row = [lax.div(v, 2) for v in ys]
        self.y_col = [2 * lax.rem(v, 2) for v in ys]
        self.z_col = [4 * lax.rem(z + d, 4) for d in range(4)]
        self.core = [core, 1 - core]

    def at(self, o):
        return self.x_row[o[0]] + self.y_row[o[1]], self.z_col[o[2]] + self.y_col[o[1]] + self.core[o[3]]

    def back(self, o):
        row, col = self.at((-o[0] % 4, -o[1] % 4, -o[2] % 4, o[3]))
        return row * COLS + col


def distance(o):
    return HOPS[o[0]] + HOPS[o[1]] + HOPS[o[2]] + 0.25 * o[3]


def exchange(
    old, ids, q_own, relaid, p_recv, s_recv,
    stage, send, recv, ids_s, ids_v, q_mine, q_all, w_rows, w, part, own_part, p_send, s_send,
    inv_v, inv_s, slot_s, from_s, here_s,
    in_sem, ids_sem, inv_sem, q_sem, q_ssem, q_rsem, ssem, rsem, o_ssem, o_rsem, p_ssem, p_rsem, s_ssem, s_rsem,
):
    here = Place()
    row, col, me = here.row, here.col, here.me

    def remote(src, dst, send_sem, recv_sem, to):
        return pltpu.make_async_remote_copy(
            src_ref=src, dst_ref=dst, send_sem=send_sem, recv_sem=recv_sem, device_id=to, device_id_type=MESH
        )

    ids_copy = pltpu.make_async_copy(ids, ids_s, ids_sem.at[0])
    ids_copy2 = pltpu.make_async_copy(ids, ids_v, ids_sem.at[1])
    q_copy = pltpu.make_async_copy(q_own, q_mine, q_sem)
    ids_copy.start()
    loads = []
    for j in range(ROWS):
        loads.append(pltpu.make_async_copy(old.at[j], stage.at[j], in_sem.at[j]))
        loads[-1].start()
    q_copy.start()
    ids_copy2.start()

    barrier = pltpu.get_barrier_semaphore()
    for o in sorted(ORDER[:-1], key=distance, reverse=True):
        pl.semaphore_signal(barrier, inc=1, device_id=here.at(o), device_id_type=MESH)

    ids_copy.wait()
    for k in range(ROWS):
        slot = jnp.int32(0)
        for j in range(ROWS):
            slot += jnp.where(lax.shift_right_arithmetic(ids_s[j, me], 7) == k, j, 0)
        slot_s[k] = lax.bitwise_and(slot, 7)

    for load in loads:
        load.wait()

    for n, o in enumerate(ORDER):
        r, c = here.at(o)
        send[n] = stage[slot_s[r], :, pl.ds(pl.multiple_of(c * 1024, 1024), 1024)]

    def send_blocks(first, last):
        for n in range(first, last):
            remote(send.at[n], recv.at[n], ssem, rsem.at[n // CHUNK], here.at(ORDER[n])).start()

    q_copy.wait()
    pl.semaphore_wait(barrier, DEVS - 1)
    for dx, a in [(2, 1), (1, 1), (3, 1), (2, 0), (0, 1), (1, 0), (3, 0)]:
        remote(q_mine, q_all.at[row], q_ssem, q_rsem, here.at((dx, 2 * a, 0, 0))).start()
    send_blocks(0, EARLY)

    q_all[row] = q_mine[...]
    recv[DEVS - 1] = send[DEVS - 1]

    ids_copy2.wait()
    held = ids_v[...]
    mine = lax.shift_right_arithmetic(held, 7) == row
    where_to = jnp.sum(jnp.where(mine, lax.bitwise_and(held, 127), 0), axis=0, keepdims=True)
    spread = jnp.transpose(jnp.broadcast_to(where_to, (DEVS, DEVS)))
    lanes = lax.broadcasted_iota(jnp.int32, (DEVS, DEVS), 1)
    sources = lax.broadcasted_iota(jnp.int32, (DEVS, DEVS), 0)
    inverse = jnp.sum(jnp.where(spread == lanes, sources, 0), axis=0, keepdims=True)
    inv_v[...] = jnp.broadcast_to(lax.bitwise_and(inverse, 127), (8, DEVS))
    inv_copy = pltpu.make_async_copy(inv_v, inv_s, inv_sem)
    inv_copy.start()
    for n, o in enumerate(ORDER):
        from_s[here.back(o)] = n

    remote(q_all.at[pl.ds(0, ROWS - 1)], q_all.at[pl.ds(0, ROWS - 1)], q_ssem, q_rsem, (row, col)).wait()
    for r in range(ROWS):
        for i in range(4):
            w_rows[32 * i + 4 * r : 32 * i + 4 * r + 4, :] = q_all[r]
    w_all = jnp.transpose(w_rows[...])
    w_high = w_all.astype(jnp.bfloat16)
    w[:, 0:128] = w_high
    w[:, 128:256] = (w_all - w_high.astype(jnp.float32)).astype(jnp.bfloat16)

    def multiply(rows, to):
        high = rows.astype(jnp.bfloat16)
        low = (rows - high.astype(jnp.float32)).astype(jnp.bfloat16)
        first = jnp.dot(high, w[...], preferred_element_type=jnp.float32)
        second = jnp.dot(low, w[:, 0:128], preferred_element_type=jnp.float32)
        product = first[:, 0:128] + (first[:, 128:256] + second)
        squares = jnp.sum(rows * rows, axis=1, keepdims=True)
        for j in range(CHUNK):
            to(j, product[8 * j : 8 * j + 8], jnp.broadcast_to(squares[8 * j : 8 * j + 8], (8, 128)))

    home = DEVS - CHUNK

    def keep_own(j, product, squares):
        own_part[j, 0] = product
        own_part[j, 1] = squares

    multiply(send[home:DEVS].reshape(CHUNK * 8, 1024), keep_own)
    part[DEVS - 1] = own_part[CHUNK - 1]
    for j in range(CHUNK - 1):
        remote(own_part.at[j], part.at[home + j], o_ssem, o_rsem, here.at(ORDER[home + j])).start()
    send_blocks(EARLY, DEVS - 1)

    inv_copy.wait()

    @pl.loop(0, DEVS, unroll=8)
    def _(p):
        here_s[p] = from_s[inv_s[0, p]]

    def arrived(i, count):
        v = recv.at[pl.ds(0, count)]
        remote(v, v, ssem, rsem.at[i], (row, col)).wait_recv()

    @pl.loop(0, CHUNKS - 1)
    def _(i):
        arrived(i, CHUNK)

        def keep(j, product, squares):
            part[i * CHUNK + j, 0] = product
            part[i * CHUNK + j, 1] = squares

        multiply(recv[pl.ds(i * CHUNK, CHUNK)].reshape(CHUNK * 8, 1024), keep)

    o7 = part.at[pl.ds(0, CHUNK - 1)]
    remote(o7, o7, o_ssem, o_rsem, (row, col)).wait()

    lane = lax.broadcasted_iota(jnp.int32, (8, 128), 1)
    sublane = lax.broadcasted_iota(jnp.int32, (8, 128), 0)
    diagonal = (lax.rem(lane, 8) == sublane) & (lane < 64)

    @pl.loop(0, COLS)
    def _(c):
        for t in range(2):
            tile = part[here_s[c * 8 + t * 4], 0]
            for i in range(1, 4):
                tile = jnp.where(lane < 32 * i, tile, part[here_s[c * 8 + t * 4 + i], 0])
            p_send[c, t] = tile
        tile = part[here_s[c * 8], 1]
        for i in range(1, 8):
            tile = jnp.where(lane < 8 * i, tile, part[here_s[c * 8 + i], 1])
        s_send[c] = jnp.sum(jnp.where(diagonal, tile, 0.0), axis=0, keepdims=True)

    across = [(0, b, z, k) for z in range(4) for b in range(2) for k in range(2) if (b, z, k) != (0, 0, 0)]
    for o in sorted(across, key=distance, reverse=True):
        c = here.z_col[o[2]] + here.y_col[o[1]] + here.core[o[3]]
        remote(p_send.at[c], p_recv.at[col], p_ssem, p_rsem, (row, c)).start()
        remote(s_send.at[c], s_recv.at[col], s_ssem, s_rsem, (row, c)).start()

    p_recv[col] = p_send[col]
    s_recv[col] = s_send[col]
    arrived(CHUNKS - 1, CHUNK - 1)

    @pl.loop(0, DEVS, unroll=8)
    def _(p):
        relaid[p] = recv[here_s[p]]

    p15 = p_recv.at[pl.ds(0, COLS - 1)]
    remote(p15, p15, p_ssem, p_rsem, (row, col)).wait()
    s15 = s_recv.at[pl.ds(0, COLS - 1)]
    remote(s15, s15, s_ssem, s_rsem, (row, col)).wait()
    v = recv.at[pl.ds(0, DEVS - 1)]
    remote(v, v, ssem, rsem.at[0], (row, col)).wait_send()


PIECES = 4


def finish(block, shares, squares, relaid, p_out, norm_out, sem):
    step = DEVS // PIECES
    copies = [
        pltpu.make_async_copy(block.at[pl.ds(i * step, step)], relaid.at[pl.ds(i * step, step)], sem.at[i])
        for i in range(PIECES)
    ]
    for copy in copies:
        copy.start()
    total, square = shares[0], squares[0]
    for c in range(1, COLS):
        total, square = total + shares[c], square + squares[c]
    norm_out[...] = jnp.sqrt(square[:, 0:64] / 16384.0 + epsilon)
    rows = []
    for g in range(8):
        t, i = divmod(g, 4)
        rows.append(total[t] if i == 0 else pltpu.roll(total[t], 128 - 32 * i, axis=1))
    p_out[...] = jnp.transpose(jnp.concatenate(rows + rows, axis=0))[0:32, 0:64]
    for copy in copies:
        copy.wait()


def on_device(old_residual, group_map, q_factor):
    f32, i32 = jnp.float32, jnp.int32
    hbm = pl.BlockSpec(memory_space=pltpu.HBM)
    vmem = pl.BlockSpec(memory_space=pltpu.VMEM)
    dma = pltpu.SemaphoreType.DMA
    given = [
        pltpu.with_memory_space_constraint(a, pltpu.HBM)
        for a in (old_residual.reshape(ROWS, 8, 16384), group_map.T, q_factor.T)
    ]
    block, shares, squares = pl.pallas_call(
        exchange,
        out_shape=(
            jax.ShapeDtypeStruct((DEVS, 8, 1024), f32),
            jax.ShapeDtypeStruct((COLS, 2, 8, 128), f32),
            jax.ShapeDtypeStruct((COLS, 1, 128), f32),
        ),
        in_specs=[hbm, hbm, hbm],
        out_specs=(vmem, vmem, vmem),
        scratch_shapes=[
            pltpu.VMEM((ROWS, 8, 16384), f32),
            pltpu.VMEM((DEVS, 8, 1024), f32),
            pltpu.VMEM((DEVS, 8, 1024), f32),
            pltpu.SMEM((8, 128), i32),
            pltpu.VMEM((8, 128), i32),
            pltpu.VMEM((4, 1024), f32),
            pltpu.VMEM((ROWS, 4, 1024), f32),
            pltpu.VMEM((128, 1024), f32),
            pltpu.VMEM((1024, 256), jnp.bfloat16),
            pltpu.VMEM((DEVS, 2, 8, 128), f32),
            pltpu.VMEM((CHUNK, 2, 8, 128), f32),
            pltpu.VMEM((COLS, 2, 8, 128), f32),
            pltpu.VMEM((COLS, 1, 128), f32),
            pltpu.VMEM((8, 128), i32),
            pltpu.SMEM((8, 128), i32),
            pltpu.SMEM((ROWS,), i32),
            pltpu.SMEM((DEVS,), i32),
            pltpu.SMEM((DEVS,), i32),
            dma((COLS,)),
            dma((2,)),
            dma,
            dma,
            dma,
            dma,
            dma,
            dma((CHUNKS,)),
            dma,
            dma,
            dma,
            dma,
            dma,
            dma,
        ],
        compiler_params=pltpu.CompilerParams(
            collective_id=0, has_side_effects=True, vmem_limit_bytes=40 << 20
        ),
    )(*given)
    relaid, projection, norms = pl.pallas_call(
        finish,
        out_shape=(
            jax.ShapeDtypeStruct((DEVS, 8, 1024), f32),
            jax.ShapeDtypeStruct((32, 64), f32),
            jax.ShapeDtypeStruct((1, 64), f32),
        ),
        in_specs=[vmem, vmem, vmem],
        out_specs=(hbm, vmem, vmem),
        scratch_shapes=[dma((PIECES,))],
        compiler_params=pltpu.CompilerParams(vmem_limit_bytes=16 << 20),
    )(block, shares, squares)
    return relaid.reshape(1024, 1024), projection, norms.reshape(64)


def solution(mesh):
    return jax.shard_map(
        on_device,
        mesh=mesh,
        in_specs=(P(("row", "col"), None), P(), P("col", "row")),
        out_specs=(P("row", "col"), P(None, ("row", "col")), P(("row", "col"))),
        check_vma=False,
    )
```

time: 126 us -> 67.6 us (0.54)
  Pallas kernels: 0 us -> 66.9 us
  waiting for transfers between devices: 54.6 us -> 0 us
  starting transfers between devices: 29.1 us -> 0 us
  other arithmetic: 18.6 us -> 0 us
  local copies, waits for them, and re-layouts: 14.8 us -> 0 us
  matrix products: 7.39 us -> 0 us
    pallas_call x0 -> x2, Pallas kernels: none -> 66.9 us  [the longest x1 64.2 us: on_device(): pl.pallas_call(exchange, out_shape=(jax.ShapeDtypeStruct((DEVS, 8, 1024),...]
    all_to_all x4 -> x0, waiting for transfers between devices: 54.6 us -> none  [the longest x1 49.1 us: on_device(): lax.all_to_all(flat_pieces, ('row', 'col'), split_axis=0, concat_axis=0,...]
    all_to_all x4 -> x0, starting transfers between devices: 29.1 us -> none  [the longest x1 11.7 us: on_device(): lax.all_to_all(flat_pieces, ('row', 'col'), split_axis=0, concat_axis=0,...]
    gather x2 -> x0, local copies, waits for them, and re-layouts: 9.99 us -> none  [the longest x1 5.02 us: on_device(): jnp.take(old_residual.reshape(row_count, group_rows, full_width), sending...]
    select_n x4 -> x0, other arithmetic: 9.82 us -> none  [the longest x2 5.11 us: on_device(): jnp.take(old_residual.reshape(row_count, group_rows, full_width), sending...]
    dot_general x1 -> x0, matrix products: 7.39 us -> none  [on_device(): jnp.dot(relaid_block, factor_full, precision=lax.Precision.HIGHEST, prefe...]
    sort x3 -> x0, other arithmetic: 4.15 us -> none  [the longest x1 2.54 us: on_device(): placement = jnp.argsort(arriving_ids)]
    reduce_sum x3 -> x0, other arithmetic: 3.11 us -> none  [the longest x1 2.45 us: on_device(): squares = jnp.sum(relaid_block * relaid_block, axis=1)]
  transfers between devices with their start and end apart: 4 -> 0, of which waited for: 2 -> 0; matrix products, arithmetic and copies ran while one was open for 19% -> 0% of each run, Pallas kernels for 0% -> 0%
where the time goes in v2:
time: 67.6 us; the launch traced here: 67.5 us
  Pallas kernels  66.9 us (99%)
    pallas_call x1, Pallas kernels, on_device(): pl.pallas_call(exchange, out_shape=(jax.ShapeDtypeStruct((DEVS, 8, 1024),...  64.2 us
    pallas_call x1, Pallas kernels, on_device(): pl.pallas_call(finish, out_shape=(jax.ShapeDtypeStruct((DEVS, 8, 1024), f...  2.65 us

profile of v2, /device:TPU:1, one launch (start us, length us, event | category | flops | bytes accessed | tf_op | source)
XLA Modules:
  0.0 67.5 jit_solution(14776813649941657806)
XLA Ops:
  0.6 64.2 %shard_map.58 = (f32[128,8,1024]{2,1,0:T(8,128)S(1)}, f32[16,2,8,128]{3,2,1,0:T(8,128)S(1)}, f32[16,1,128]{2,1,0:T(1,128)S(1)}) custom-call(f32[8,8,16384]{2,1,0:T(8,128)} %bitcast.5, s32[8,128]{1,0:T(8,128)} %bitcast.7, f32[4,1024]{1,0:T(4,128)} %bitcast.6), custom_call_target="tpu_custom_call" | custom-call | tf_op jit(solution)/shard_map/pallas_call | solution.py:253
  64.9 2.7 %shard_map.59 = (f32[128,8,1024]{2,1,0:T(8,128)}, f32[32,64]{1,0:T(8,128)}, f32[1,64]{1,0:T(1,128)}) custom-call(f32[128,8,1024]{2,1,0:T(8,128)S(1)} %get-tuple-element.9.block, f32[16,2,8,128]{3,2,1,0:T(8,128)S(1)} %get-tuple-element.10.shares, f32[16,1,128]{2,1,0:T(1,128)S(1)} %get-tuple-element.11.squares), custom_call_target="tpu_custom_call" | custom-call | tf_op jit(solution)/shard_map/pallas_call | solution.py:300

commit v3 on v2

--- a/solution.py
+++ b/solution.py
@@ -9,8 +9,9 @@
 MESH = pl.DeviceIdType.MESH
 ROWS, COLS = 8, 16
 DEVS = ROWS * COLS
-CHUNK = 8
-CHUNKS = DEVS // CHUNK
+BULK = DEVS - ROWS
+CHUNK = 24
+CHUNKS = BULK // CHUNK
 
 
 def order():
@@ -20,9 +21,14 @@
         s = MULT_S * (n + 1) % ROWS
         v = {name: c >> i & 1 for i, name in enumerate(BITS_C)} | {name: s >> i & 1 for i, name in enumerate(BITS_S)}
         offsets.append((v["x0"] + 2 * v["x1"], v["y0"] + 2 * v["y1"], v["z0"] + 2 * v["z1"], v["k"]))
-    return offsets
-
-
+    axes = lambda o: sum(1 for d in o[:3] if d)
+    spread = lambda group, count: [group[len(group) * i // count] for i in range(count)]
+    first = spread([o for o in offsets[: DEVS - ROWS] if axes(o) < 2], NEAR)
+    second = spread([o for o in offsets[: DEVS - ROWS] if axes(o) == 2], PLANE)
+    return first + second + [o for o in offsets if o not in first + second]
+
+
+NEAR, PLANE = 15, 16
 MULT_C, MULT_S = 7, 3
 BITS_C, BITS_S = ("z0", "z1", "y0", "k"), ("x0", "x1", "y1")
 EARLY = 96
@@ -57,9 +63,9 @@
 
 def exchange(
     old, ids, q_own, relaid, p_recv, s_recv,
-    stage, send, recv, ids_s, ids_v, q_mine, q_all, w_rows, w, part, own_part, p_send, s_send,
+    stage, send, recv, ids_s, ids_v, q_mine, q_all, w_rows, w, part, p_send, s_send,
     inv_v, inv_s, slot_s, from_s, here_s,
-    in_sem, ids_sem, inv_sem, q_sem, q_ssem, q_rsem, ssem, rsem, o_ssem, o_rsem, p_ssem, p_rsem, s_ssem, s_rsem,
+    in_sem, ids_sem, inv_sem, q_sem, q_ssem, q_rsem, ssem, rsem, p_ssem, p_rsem, s_ssem, s_rsem, tree,
 ):
     here = Place()
     row, col, me = here.row, here.col, here.me
@@ -81,9 +87,16 @@
     ids_copy2.start()
 
     barrier = pltpu.get_barrier_semaphore()
-    for o in sorted(ORDER[:-1], key=distance, reverse=True):
+    lines = [(d, 0, 0, k) for d in range(4) for k in range(2) if d or k]
+    lines += [(0, d, 0, k) for d in range(1, 4) for k in range(2)]
+    lines += [(0, 0, d, k) for d in range(1, 4) for k in range(2)]
+    for o in sorted(lines, key=distance, reverse=True):
         pl.semaphore_signal(barrier, inc=1, device_id=here.at(o), device_id_type=MESH)
 
+    pl.semaphore_wait(barrier, len(lines))
+    for d in (2, 1, 3):
+        pl.semaphore_signal(tree.at[0], inc=1, device_id=here.at((d, 0, 0, 0)), device_id_type=MESH)
+        pl.semaphore_signal(tree.at[0], inc=1, device_id=here.at((0, d, 0, 0)), device_id_type=MESH)
     ids_copy.wait()
     for k in range(ROWS):
         slot = jnp.int32(0)
@@ -94,19 +107,34 @@
     for load in loads:
         load.wait()
 
-    for n, o in enumerate(ORDER):
-        r, c = here.at(o)
-        send[n] = stage[slot_s[r], :, pl.ds(pl.multiple_of(c * 1024, 1024), 1024)]
+    def arrange(first, last):
+        for n in range(first, last):
+            r, c = here.at(ORDER[n])
+            send[n] = stage[slot_s[r], :, pl.ds(pl.multiple_of(c * 1024, 1024), 1024)]
+
+    arrange(0, NEAR)
 
     def send_blocks(first, last):
         for n in range(first, last):
-            remote(send.at[n], recv.at[n], ssem, rsem.at[n // CHUNK], here.at(ORDER[n])).start()
+            remote(send.at[n], recv.at[n], ssem, rsem.at[min(n // CHUNK, CHUNKS)], here.at(ORDER[n])).start()
 
     q_copy.wait()
-    pl.semaphore_wait(barrier, DEVS - 1)
-    for dx, a in [(2, 1), (1, 1), (3, 1), (2, 0), (0, 1), (1, 0), (3, 0)]:
-        remote(q_mine, q_all.at[row], q_ssem, q_rsem, here.at((dx, 2 * a, 0, 0))).start()
-    send_blocks(0, EARLY)
+    remote(q_mine, q_all.at[row], q_ssem, q_rsem.at[0], here.at((0, 2, 0, 0))).start()
+    for d in (2, 1, 3):
+        remote(q_mine, q_all.at[row], q_ssem, q_rsem.at[1], here.at((d, 0, 0, 0))).start()
+    send_blocks(0, NEAR)
+    arrange(NEAR, DEVS)
+    pl.semaphore_wait(tree.at[0], 6)
+    for d in (2, 1, 3):
+        pl.semaphore_signal(tree.at[1], inc=1, device_id=here.at((d, 0, 0, 0)), device_id_type=MESH)
+    send_blocks(NEAR, NEAR + PLANE)
+    partner = here.at((0, 2, 0, 0))[0]
+    remote(q_mine, q_all.at[partner], q_ssem, q_rsem.at[0], (row, col)).wait_recv()
+    for d in (2, 1, 3):
+        remote(q_all.at[partner], q_all.at[partner], q_ssem, q_rsem.at[2], here.at((d, 0, 0, 0))).start()
+    pl.semaphore_wait(tree.at[1], 3)
+    send_blocks(NEAR + PLANE, EARLY)
+    send_blocks(EARLY, DEVS - 1)
 
     q_all[row] = q_mine[...]
     recv[DEVS - 1] = send[DEVS - 1]
@@ -125,7 +153,10 @@
     for n, o in enumerate(ORDER):
         from_s[here.back(o)] = n
 
-    remote(q_all.at[pl.ds(0, ROWS - 1)], q_all.at[pl.ds(0, ROWS - 1)], q_ssem, q_rsem, (row, col)).wait()
+    q7, q3 = q_all.at[pl.ds(0, ROWS - 1)], q_all.at[pl.ds(0, 3)]
+    remote(q3, q3, q_ssem, q_rsem.at[1], (row, col)).wait_recv()
+    remote(q3, q3, q_ssem, q_rsem.at[2], (row, col)).wait_recv()
+    remote(q7, q7, q_ssem, q_rsem.at[2], (row, col)).wait_send()
     for r in range(ROWS):
         for i in range(4):
             w_rows[32 * i + 4 * r : 32 * i + 4 * r + 4, :] = q_all[r]
@@ -141,20 +172,8 @@
         second = jnp.dot(low, w[:, 0:128], preferred_element_type=jnp.float32)
         product = first[:, 0:128] + (first[:, 128:256] + second)
         squares = jnp.sum(rows * rows, axis=1, keepdims=True)
-        for j in range(CHUNK):
+        for j in range(rows.shape[0] // 8):
             to(j, product[8 * j : 8 * j + 8], jnp.broadcast_to(squares[8 * j : 8 * j + 8], (8, 128)))
-
-    home = DEVS - CHUNK
-
-    def keep_own(j, product, squares):
-        own_part[j, 0] = product
-        own_part[j, 1] = squares
-
-    multiply(send[home:DEVS].reshape(CHUNK * 8, 1024), keep_own)
-    part[DEVS - 1] = own_part[CHUNK - 1]
-    for j in range(CHUNK - 1):
-        remote(own_part.at[j], part.at[home + j], o_ssem, o_rsem, here.at(ORDER[home + j])).start()
-    send_blocks(EARLY, DEVS - 1)
 
     inv_copy.wait()
 
@@ -166,44 +185,55 @@
         v = recv.at[pl.ds(0, count)]
         remote(v, v, ssem, rsem.at[i], (row, col)).wait_recv()
 
-    @pl.loop(0, CHUNKS - 1)
+    def product(first, count):
+        def keep(j, product, squares):
+            part[first + j, 0] = product
+            part[first + j, 1] = squares
+
+        multiply(recv[pl.ds(first, count)].reshape(count * 8, 1024), keep)
+
+    @pl.loop(0, CHUNKS)
     def _(i):
         arrived(i, CHUNK)
-
-        def keep(j, product, squares):
-            part[i * CHUNK + j, 0] = product
-            part[i * CHUNK + j, 1] = squares
-
-        multiply(recv[pl.ds(i * CHUNK, CHUNK)].reshape(CHUNK * 8, 1024), keep)
-
-    o7 = part.at[pl.ds(0, CHUNK - 1)]
-    remote(o7, o7, o_ssem, o_rsem, (row, col)).wait()
+        product(i * CHUNK, CHUNK)
+
+    arrived(CHUNKS, ROWS - 1)
+    product(BULK, ROWS)
 
     lane = lax.broadcasted_iota(jnp.int32, (8, 128), 1)
     sublane = lax.broadcasted_iota(jnp.int32, (8, 128), 0)
     diagonal = (lax.rem(lane, 8) == sublane) & (lane < 64)
 
-    @pl.loop(0, COLS)
-    def _(c):
+    def gather(c, p_to, s_to):
         for t in range(2):
             tile = part[here_s[c * 8 + t * 4], 0]
             for i in range(1, 4):
                 tile = jnp.where(lane < 32 * i, tile, part[here_s[c * 8 + t * 4 + i], 0])
-            p_send[c, t] = tile
+            p_to[t] = tile
         tile = part[here_s[c * 8], 1]
         for i in range(1, 8):
             tile = jnp.where(lane < 8 * i, tile, part[here_s[c * 8 + i], 1])
-        s_send[c] = jnp.sum(jnp.where(diagonal, tile, 0.0), axis=0, keepdims=True)
+        s_to[...] = jnp.sum(jnp.where(diagonal, tile, 0.0), axis=0, keepdims=True)
 
     across = [(0, b, z, k) for z in range(4) for b in range(2) for k in range(2) if (b, z, k) != (0, 0, 0)]
-    for o in sorted(across, key=distance, reverse=True):
-        c = here.z_col[o[2]] + here.y_col[o[1]] + here.core[o[3]]
-        remote(p_send.at[c], p_recv.at[col], p_ssem, p_rsem, (row, c)).start()
-        remote(s_send.at[c], s_recv.at[col], s_ssem, s_rsem, (row, c)).start()
-
-    p_recv[col] = p_send[col]
-    s_recv[col] = s_send[col]
-    arrived(CHUNKS - 1, CHUNK - 1)
+    across = sorted(across, key=distance, reverse=True)
+
+    def column(o):
+        return here.z_col[o[2]] + here.y_col[o[1]] + here.core[o[3]]
+
+    def share(some):
+        for o in some:
+            c = column(o)
+            remote(p_send.at[c], p_recv.at[col], p_ssem, p_rsem, (row, c)).start()
+            remote(s_send.at[c], s_recv.at[col], s_ssem, s_rsem, (row, c)).start()
+
+    for first in range(0, 16, 4):
+        for o in across[first : first + 4]:
+            gather(column(o), p_send.at[column(o)], s_send.at[column(o)])
+        if first:
+            share(across[first - 4 : first])
+    share(across[12:])
+    gather(col, p_recv.at[col], s_recv.at[col])
 
     @pl.loop(0, DEVS, unroll=8)
     def _(p):
@@ -220,7 +250,7 @@
 PIECES = 4
 
 
-def finish(block, shares, squares, relaid, p_out, norm_out, sem):
+def finish(block, shares, squares, relaid, p_out, norm_out, p_done, norm_done, sem, small_sem):
     step = DEVS // PIECES
     copies = [
         pltpu.make_async_copy(block.at[pl.ds(i * step, step)], relaid.at[pl.ds(i * step, step)], sem.at[i])
@@ -231,13 +261,19 @@
     total, square = shares[0], squares[0]
     for c in range(1, COLS):
         total, square = total + shares[c], square + squares[c]
-    norm_out[...] = jnp.sqrt(square[:, 0:64] / 16384.0 + epsilon)
+    norm_done[...] = jnp.sqrt(square[:, 0:64] / 16384.0 + epsilon)
     rows = []
     for g in range(8):
         t, i = divmod(g, 4)
         rows.append(total[t] if i == 0 else pltpu.roll(total[t], 128 - 32 * i, axis=1))
-    p_out[...] = jnp.transpose(jnp.concatenate(rows + rows, axis=0))[0:32, 0:64]
-    for copy in copies:
+    p_done[...] = jnp.transpose(jnp.concatenate(rows + rows, axis=0))[0:32, 0:64]
+    small = [
+        pltpu.make_async_copy(norm_done, norm_out, small_sem.at[0]),
+        pltpu.make_async_copy(p_done, p_out, small_sem.at[1]),
+    ]
+    for copy in small:
+        copy.start()
+    for copy in copies + small:
         copy.wait()
 
 
@@ -270,7 +306,6 @@
             pltpu.VMEM((128, 1024), f32),
             pltpu.VMEM((1024, 256), jnp.bfloat16),
             pltpu.VMEM((DEVS, 2, 8, 128), f32),
-            pltpu.VMEM((CHUNK, 2, 8, 128), f32),
             pltpu.VMEM((COLS, 2, 8, 128), f32),
             pltpu.VMEM((COLS, 1, 128), f32),
             pltpu.VMEM((8, 128), i32),
@@ -283,15 +318,14 @@
             dma,
             dma,
             dma,
-            dma,
-            dma,
-            dma((CHUNKS,)),
-            dma,
-            dma,
-            dma,
-            dma,
-            dma,
-            dma,
+            dma((3,)),
+            dma,
+            dma((CHUNKS + 1,)),
+            dma,
+            dma,
+            dma,
+            dma,
+            pltpu.SemaphoreType.REGULAR((2,)),
         ],
         compiler_params=pltpu.CompilerParams(
             collective_id=0, has_side_effects=True, vmem_limit_bytes=40 << 20
@@ -305,8 +339,8 @@
             jax.ShapeDtypeStruct((1, 64), f32),
         ),
         in_specs=[vmem, vmem, vmem],
-        out_specs=(hbm, vmem, vmem),
-        scratch_shapes=[dma((PIECES,))],
+        out_specs=(hbm, hbm, hbm),
+        scratch_shapes=[pltpu.VMEM((32, 64), f32), pltpu.VMEM((1, 64), f32), dma((PIECES,)), dma((2,))],
         compiler_params=pltpu.CompilerParams(vmem_limit_bytes=16 << 20),
     )(block, shares, squares)
     return relaid.reshape(1024, 1024), projection, norms.reshape(64)

time: 67.6 us -> 65.4 us (0.967)
  Pallas kernels: 66.9 us -> 64.7 us
    pallas_call x1, Pallas kernels: 64.2 us -> 62.6 us  [on_device(): pl.pallas_call(exchange, out_shape=(jax.ShapeDtypeStruct((DEVS, 8, 1024),...]
where the time goes in v3:
time: 65.4 us; the launch traced here: 65.3 us
  Pallas kernels  64.7 us (99%)
    pallas_call x1, Pallas kernels, on_device(): pl.pallas_call(exchange, out_shape=(jax.ShapeDtypeStruct((DEVS, 8, 1024),...  62.6 us
    pallas_call x1, Pallas kernels, on_device(): pl.pallas_call(finish, out_shape=(jax.ShapeDtypeStruct((DEVS, 8, 1024), f...  2.06 us

profile of v3, /device:TPU:1, one launch (start us, length us, event | category | flops | bytes accessed | tf_op | source)
XLA Modules:
  0.0 65.3 jit_solution(3861225003104877532)
XLA Ops:
  0.6 62.6 %shard_map.58 = (f32[128,8,1024]{2,1,0:T(8,128)S(1)}, f32[16,2,8,128]{3,2,1,0:T(8,128)S(1)}, f32[16,1,128]{2,1,0:T(1,128)S(1)}) custom-call(f32[8,8,16384]{2,1,0:T(8,128)} %bitcast.5, s32[8,128]{1,0:T(8,128)} %bitcast.7, f32[4,1024]{1,0:T(4,128)} %bitcast.6), custom_call_target="tpu_custom_call" | custom-call | tf_op jit(solution)/shard_map/pallas_call | solution.py:289
  63.3 2.1 %shard_map.59 = (f32[128,8,1024]{2,1,0:T(8,128)}, f32[32,64]{1,0:T(8,128)}, f32[1,64]{1,0:T(1,128)}) custom-call(f32[128,8,1024]{2,1,0:T(8,128)S(1)} %get-tuple-element.9.block, f32[16,2,8,128]{3,2,1,0:T(8,128)S(1)} %get-tuple-element.10.shares, f32[16,1,128]{2,1,0:T(1,128)S(1)} %get-tuple-element.11.squares), custom_call_target="tpu_custom_call" | custom-call | tf_op jit(solution)/shard_map/pallas_call | solution.py:334

commit v4 on v3

--- a/solution.py
+++ b/solution.py
@@ -25,10 +25,12 @@
     spread = lambda group, count: [group[len(group) * i // count] for i in range(count)]
     first = spread([o for o in offsets[: DEVS - ROWS] if axes(o) < 2], NEAR)
     second = spread([o for o in offsets[: DEVS - ROWS] if axes(o) == 2], PLANE)
-    return first + second + [o for o in offsets if o not in first + second]
-
-
-NEAR, PLANE = 15, 16
+    rest = [o for o in offsets[: DEVS - ROWS] if o not in first + second]
+    far = lambda o: -sum((0, 1, 2, 1)[d] for d in o[:3])
+    return first + second + rest[:-12] + sorted(rest[-12:], key=far) + sorted(offsets[DEVS - ROWS :], key=far)
+
+
+NEAR, PLANE = 15, 12
 MULT_C, MULT_S = 7, 3
 BITS_C, BITS_S = ("z0", "z1", "y0", "k"), ("x0", "x1", "y1")
 EARLY = 96

time: 65.4 us -> 64.6 us (0.988)
  Pallas kernels: 64.7 us -> 63.9 us
    pallas_call x1, Pallas kernels: 62.6 us -> 61.8 us  [on_device(): pl.pallas_call(exchange, out_shape=(jax.ShapeDtypeStruct((DEVS, 8, 1024),...]
where the time goes in v4:
time: 64.6 us; the launch traced here: 64.5 us
  Pallas kernels  63.9 us (99%)
    pallas_call x1, Pallas kernels, on_device(): pl.pallas_call(exchange, out_shape=(jax.ShapeDtypeStruct((DEVS, 8, 1024),...  61.8 us
    pallas_call x1, Pallas kernels, on_device(): pl.pallas_call(finish, out_shape=(jax.ShapeDtypeStruct((DEVS, 8, 1024), f...  2.06 us

profile of v4, /device:TPU:1, one launch (start us, length us, event | category | flops | bytes accessed | tf_op | source)
XLA Modules:
  0.0 64.5 jit_solution(2462821494444693459)
XLA Ops:
  0.6 61.8 %shard_map.58 = (f32[128,8,1024]{2,1,0:T(8,128)S(1)}, f32[16,2,8,128]{3,2,1,0:T(8,128)S(1)}, f32[16,1,128]{2,1,0:T(1,128)S(1)}) custom-call(f32[8,8,16384]{2,1,0:T(8,128)} %bitcast.5, s32[8,128]{1,0:T(8,128)} %bitcast.7, f32[4,1024]{1,0:T(4,128)} %bitcast.6), custom_call_target="tpu_custom_call" | custom-call | tf_op jit(solution)/shard_map/pallas_call | solution.py:291
  62.4 2.1 %shard_map.59 = (f32[128,8,1024]{2,1,0:T(8,128)}, f32[32,64]{1,0:T(8,128)}, f32[1,64]{1,0:T(1,128)}) custom-call(f32[128,8,1024]{2,1,0:T(8,128)S(1)} %get-tuple-element.9.block, f32[16,2,8,128]{3,2,1,0:T(8,128)S(1)} %get-tuple-element.10.shares, f32[16,1,128]{2,1,0:T(1,128)S(1)} %get-tuple-element.11.squares), custom_call_target="tpu_custom_call" | custom-call | tf_op jit(solution)/shard_map/pallas_call | solution.py:336

commit v5 on v4

--- a/solution.py
+++ b/solution.py
@@ -10,7 +10,7 @@
 ROWS, COLS = 8, 16
 DEVS = ROWS * COLS
 BULK = DEVS - ROWS
-CHUNK = 24
+CHUNK = 8
 CHUNKS = BULK // CHUNK
 
 
@@ -65,9 +65,9 @@
 
 def exchange(
     old, ids, q_own, relaid, p_recv, s_recv,
-    stage, send, recv, ids_s, ids_v, q_mine, q_all, w_rows, w, part, p_send, s_send,
+    stage, send, recv, ids_s, ids_v, q_mine, q_all, w_rows, w, part, own_part, own_recv, p_send, s_send,
     inv_v, inv_s, slot_s, from_s, here_s,
-    in_sem, ids_sem, inv_sem, q_sem, q_ssem, q_rsem, ssem, rsem, p_ssem, p_rsem, s_ssem, s_rsem, tree,
+    in_sem, ids_sem, inv_sem, q_sem, q_ssem, q_rsem, ssem, rsem, o_ssem, o_rsem, p_ssem, p_rsem, s_ssem, s_rsem, tree,
 ):
     here = Place()
     row, col, me = here.row, here.col, here.me
@@ -136,7 +136,6 @@
         remote(q_all.at[partner], q_all.at[partner], q_ssem, q_rsem.at[2], here.at((d, 0, 0, 0))).start()
     pl.semaphore_wait(tree.at[1], 3)
     send_blocks(NEAR + PLANE, EARLY)
-    send_blocks(EARLY, DEVS - 1)
 
     q_all[row] = q_mine[...]
     recv[DEVS - 1] = send[DEVS - 1]
@@ -177,6 +176,17 @@
         for j in range(rows.shape[0] // 8):
             to(j, product[8 * j : 8 * j + 8], jnp.broadcast_to(squares[8 * j : 8 * j + 8], (8, 128)))
 
+    lane = lax.broadcasted_iota(jnp.int32, (8, 128), 1)
+
+    def keep_own(j, product, squares):
+        own_part[j] = jnp.where(lane < 32, product, squares)
+
+    multiply(send[BULK:DEVS].reshape(ROWS * 8, 1024), keep_own)
+    own_recv[ROWS - 1] = own_part[ROWS - 1]
+    for j in range(ROWS - 1):
+        remote(own_part.at[j], own_recv.at[j], o_ssem, o_rsem, here.at(ORDER[BULK + j])).start()
+    send_blocks(EARLY, DEVS - 1)
+
     inv_copy.wait()
 
     @pl.loop(0, DEVS, unroll=8)
@@ -194,15 +204,23 @@
 
         multiply(recv[pl.ds(first, count)].reshape(count * 8, 1024), keep)
 
-    @pl.loop(0, CHUNKS)
+    @pl.loop(0, CHUNKS - 1)
     def _(i):
         arrived(i, CHUNK)
         product(i * CHUNK, CHUNK)
 
-    arrived(CHUNKS, ROWS - 1)
-    product(BULK, ROWS)
-
-    lane = lax.broadcasted_iota(jnp.int32, (8, 128), 1)
+    o7 = own_recv.at[pl.ds(0, ROWS - 1)]
+    remote(o7, o7, o_ssem, o_rsem, (row, col)).wait()
+    for j in range(ROWS):
+        both = own_recv[j]
+        once = jnp.where(lane < 32, both, 0.0)
+        twice = once + pltpu.roll(once, 32, axis=1)
+        part[BULK + j, 0] = twice + pltpu.roll(twice, 64, axis=1)
+        part[BULK + j, 1] = jnp.where(lane < 32, pltpu.roll(both, 64, axis=1), both)
+
+    arrived(CHUNKS - 1, CHUNK)
+    product(BULK - CHUNK, CHUNK)
+
     sublane = lax.broadcasted_iota(jnp.int32, (8, 128), 0)
     diagonal = (lax.rem(lane, 8) == sublane) & (lane < 64)
 
@@ -236,6 +254,7 @@
             share(across[first - 4 : first])
     share(across[12:])
     gather(col, p_recv.at[col], s_recv.at[col])
+    arrived(CHUNKS, ROWS - 1)
 
     @pl.loop(0, DEVS, unroll=8)
     def _(p):
@@ -308,6 +327,8 @@
             pltpu.VMEM((128, 1024), f32),
             pltpu.VMEM((1024, 256), jnp.bfloat16),
             pltpu.VMEM((DEVS, 2, 8, 128), f32),
+            pltpu.VMEM((ROWS, 8, 128), f32),
+            pltpu.VMEM((ROWS, 8, 128), f32),
             pltpu.VMEM((COLS, 2, 8, 128), f32),
             pltpu.VMEM((COLS, 1, 128), f32),
             pltpu.VMEM((8, 128), i32),
@@ -323,6 +344,8 @@
             dma((3,)),
             dma,
             dma((CHUNKS + 1,)),
+            dma,
+            dma,
             dma,
             dma,
             dma,

time: 64.6 us -> 64.8 us (level); the launches traced: 64.5 us -> 63.9 us
  Pallas kernels: 63.9 us -> 63.2 us
where the time goes in v5:
time: 64.8 us; the launch traced here: 63.9 us
  Pallas kernels  63.2 us (98%)
    pallas_call x1, Pallas kernels, on_device(): pl.pallas_call(exchange, out_shape=(jax.ShapeDtypeStruct((DEVS, 8, 1024),...  61.2 us
    pallas_call x1, Pallas kernels, on_device(): pl.pallas_call(finish, out_shape=(jax.ShapeDtypeStruct((DEVS, 8, 1024), f...  2.06 us

profile of v5, /device:TPU:1, one launch (start us, length us, event | category | flops | bytes accessed | tf_op | source)
XLA Modules:
  0.0 63.9 jit_solution(4474124333054080846)
XLA Ops:
  0.6 61.2 %shard_map.58 = (f32[128,8,1024]{2,1,0:T(8,128)S(1)}, f32[16,2,8,128]{3,2,1,0:T(8,128)S(1)}, f32[16,1,128]{2,1,0:T(1,128)S(1)}) custom-call(f32[8,8,16384]{2,1,0:T(8,128)} %bitcast.5, s32[8,128]{1,0:T(8,128)} %bitcast.7, f32[4,1024]{1,0:T(4,128)} %bitcast.6), custom_call_target="tpu_custom_call" | custom-call | tf_op jit(solution)/shard_map/pallas_call | solution.py:310
  61.8 2.1 %shard_map.59 = (f32[128,8,1024]{2,1,0:T(8,128)}, f32[32,64]{1,0:T(8,128)}, f32[1,64]{1,0:T(1,128)}) custom-call(f32[128,8,1024]{2,1,0:T(8,128)S(1)} %get-tuple-element.9.block, f32[16,2,8,128]{3,2,1,0:T(8,128)S(1)} %get-tuple-element.10.shares, f32[16,1,128]{2,1,0:T(1,128)S(1)} %get-tuple-element.11.squares), custom_call_target="tpu_custom_call" | custom-call | tf_op jit(solution)/shard_map/pallas_call | solution.py:359
